TPU v7x, 32 devices: a whole 2x2x4 slice. The times are simulated.
32 devices in a mesh: trait: 2 (over x), ppl: 16 (over z, y, core).
Axes of the slice: x: 2, y: 2, z: 4, core: 2. Of those that a mesh axis runs over, the one named last changes fastest.
Arguments:
- genotypes: bfloat16 [8192, 4096], P(('trait', 'ppl')), parts along dimension 0
- residual: float32 [64, 4096], P('trait', 'ppl'), parts along dimension 0, may hold values from -36 to 36
- noise_people: float32 [64, 4096], P('trait', 'ppl'), parts along dimension 0, may hold values from -6 to 6
- noise_coef: float32 [64, 4096], P('trait'), parts along dimension 0, may hold values from -6 to 6
- coef_all: float32 [64, 8192], P('trait'), parts along dimension 0, may hold values from -0.06 to 0.06
- block_index: int32 [2], P('trait'), parts along dimension 0, may hold values from 0 to 1
- prior_prec: float32 [64], P('trait'), parts along dimension 0, may hold values from 21 to 103
- sigma2_old: float32 [64], P('trait'), parts along dimension 0, may hold values from 0.5 to 2
- gamma_draw: float32 [64], P('trait'), parts along dimension 0, may hold values from 0.8 to 1.25
- valid_counts: int32 [32], P('trait'), parts along dimension 0, may hold values from 128 to 256, as said below
Outputs:
- coef_new: float32 [64, 8192], P('trait'), parts along dimension 0
- residual_new: float32 [64, 4096], P('trait', 'ppl'), parts along dimension 0
- sigma2_new: float32 [64], P('trait'), parts along dimension 0
There are 2 independent parts, one for each index of `trait`. A program takes and returns all parts, laid end to end along the dimension named above; each array names one. Nothing has to cross between parts.
Inputs may be any that keep to these rules, and one draw needn't show every extreme that they name: `valid_counts`: each entry counts the people present in one device's 256 slots; they fill the lowest slots, and some entry equals 256.
All inputs are finite; a program needn't handle non-finite values.
Results may differ from a plain program's by a relative error of at most 0.0049.
Values may be sent and summed in bfloat16 or wider, within the bound.
A program may use at most 64 MiB of HBM per device.

v0:
```python
import jax
import jax.numpy as jnp
from jax import lax
from jax.sharding import PartitionSpec as P

ITERS = 4


PRIOR_DOF = 4.0
PRIOR_SCALE = 0.5
CONTRACT = (((1,), (1,)), ((), ()))


def per_device(
    genotypes,
    residual,
    noise_people,
    noise_coef,
    coef_all,
    block_index,
    prior_prec,
    sigma2_old,
    gamma_draw,
    valid_counts,
):
    row_count = genotypes.shape[0]
    batch_width = genotypes.shape[1]
    my_shard = lax.axis_index("ppl")
    person_mask = (jnp.arange(row_count) < valid_counts[my_shard]).astype(jnp.float32)[None, :]
    first_col = block_index[0] * batch_width
    old_coef = lax.dynamic_slice_in_dim(coef_all, first_col, batch_width, 1)
    fitted_old = lax.dot_general(
        old_coef.astype(jnp.bfloat16), genotypes, CONTRACT, preferred_element_type=jnp.float32
    )
    partial_res = person_mask * (residual + fitted_old)
    noise_var = sigma2_old[:, None]
    ridge = prior_prec[:, None]
    target = (person_mask * (partial_res + jnp.sqrt(noise_var) * noise_people)).astype(jnp.bfloat16)
    data_part = jnp.dot(target, genotypes, preferred_element_type=jnp.float32)
    fitted = jnp.zeros_like(partial_res)
    rhs = lax.psum(data_part, "ppl") / noise_var + jnp.sqrt(ridge) * noise_coef
    batch_coef = jnp.zeros_like(rhs)
    search = rhs
    direction = rhs
    norm_now = jnp.sum(search * search, axis=1)
    for number in range(ITERS):
        dir_low = direction.astype(jnp.bfloat16)
        dir_full = lax.optimization_barrier(dir_low).astype(jnp.float32)
        image = person_mask * lax.dot_general(
            dir_low, genotypes, CONTRACT, preferred_element_type=jnp.float32
        )
        local_sum = jnp.dot(
            image.astype(jnp.bfloat16), genotypes, preferred_element_type=jnp.float32
        )
        local_sum = lax.psum(local_sum, "ppl")
        applied = local_sum / noise_var + ridge * dir_full
        step_size = norm_now / jnp.sum(dir_full * applied, axis=1)
        batch_coef = batch_coef + step_size[:, None] * dir_full
        fitted = fitted + step_size[:, None] * image
        search = search - step_size[:, None] * applied
        norm_next = jnp.sum(search * search, axis=1)
        direction = search + (norm_next / norm_now)[:, None] * direction
        norm_now = norm_next
    residual_new = partial_res - fitted
    squares = lax.psum(jnp.sum(residual_new * residual_new, axis=1), "ppl")
    present = jnp.sum(valid_counts).astype(jnp.float32)
    sigma2_new = (squares + PRIOR_DOF * PRIOR_SCALE) / ((present + PRIOR_DOF) * gamma_draw)
    coef_new = lax.dynamic_update_slice_in_dim(coef_all, batch_coef, first_col, 1)
    return (coef_new, residual_new, sigma2_new)


def solution(mesh):
    return jax.shard_map(
        per_device,
        mesh=mesh,
        in_specs=(
            P(("trait", "ppl"), None),
            P("trait", "ppl"),
            P("trait", "ppl"),
            P("trait", None),
            P("trait", None),
            P("trait"),
            P("trait"),
            P("trait"),
            P("trait"),
            P("trait"),
        ),
        out_specs=(P("trait", None), P("trait", "ppl"), P("trait")),
        check_vma=False,
    )
```

profile of v0, /device:TPU:0, one launch (start us, length us, event | category | flops | bytes accessed | tf_op | source)
XLA Modules:
  0.0 537.2 jit_solution(11827598137406431919)
XLA Ops:
  7.3 1.4 copy.21
  10.6 0.7 fusion
  11.4 1.3 fusion.14
  12.8 93.5 %all-reduce.6.cloned.1.call-done = f32[32,4096]{1,0:T(8,128)} async-done(((f32[32,4096]{1,0:T(8,128)}), f32[32,4096]{1,0:T(8,128)}) %all-reduce.6.cloned.1.call-update) | async-done | bytes 524304 | tf_op jit(solution)/shard_map/psum | solution.py:41
  106.3 1.5 multiply_reduce_fusion.3
  107.8 0.7 convolution_multiply_fusion.3
  108.5 1.3 fusion.21
  109.9 91.3 %all-reduce.8.cloned.1.call-done = f32[32,4096]{1,0:T(8,128)} async-done(((f32[32,4096]{1,0:T(8,128)}), f32[32,4096]{1,0:T(8,128)}) %all-reduce.8.cloned.1.call-update) | async-done | bytes 524304 | tf_op jit(solution)/shard_map/psum | solution.py:55
  201.2 1.3 fusion.2
  202.5 1.4 multiply_reduce_fusion.2
  203.9 0.8 copy-done.1
  204.8 0.7 convolution_multiply_fusion.2
  205.6 1.3 fusion.19
  206.9 91.3 %all-reduce.10.cloned.1.call-done = f32[32,4096]{1,0:T(8,128)} async-done(((f32[32,4096]{1,0:T(8,128)}), f32[32,4096]{1,0:T(8,128)}) %all-reduce.10.cloned.1.call-update) | async-done | bytes 524304 | tf_op jit(solution)/shard_map/psum | solution.py:55
  298.2 1.3 fusion.8
  299.6 1.5 multiply_reduce_fusion.1
  301.1 2.0 fusion.26
  303.1 0.7 convolution_multiply_fusion.1
  303.9 1.3 fusion.17
  305.3 91.3 %all-reduce.12.cloned.1.call-done = f32[32,4096]{1,0:T(8,128)} async-done(((f32[32,4096]{1,0:T(8,128)}), f32[32,4096]{1,0:T(8,128)}) %all-reduce.12.cloned.1.call-update) | async-done | bytes 524304 | tf_op jit(solution)/shard_map/psum | solution.py:55
  396.5 1.4 fusion.10
  397.9 0.7 div.93
  398.6 1.4 multiply_reduce_fusion
  400.0 0.7 div.94
  400.9 0.7 copy-done.7
  401.6 0.7 convolution_multiply_fusion
  402.4 1.3 fusion.15
  405.0 90.0 %all-reduce.14.cloned.1.call-done = f32[32,4096]{1,0:T(8,128)} async-done(((f32[32,4096]{1,0:T(8,128)}), f32[32,4096]{1,0:T(8,128)}) %all-reduce.14.cloned.1.call-update) | async-done | bytes 524304 | tf_op jit(solution)/shard_map/psum | solution.py:55
  495.1 1.3 fusion.12
  496.5 1.1 fusion.6
  497.5 0.8 multiply_reduce_fusion.4
  498.3 31.9 %psum.47 = f32[32]{0:T(128)S(1)} all-reduce(f32[32]{0:T(128)S(1)} %get-tuple-element.3), channel_id=1, replica_groups=mesh['trait'=2,'ppl'=16] {'ppl'}, use_global_device_ids=true, to_apply=%region_14.0 | all-reduce | flops 32 | bytes 256 | tf_op jit(solution)/shard_map/psum | solution.py:65
  (72 shorter events, 3.2 us)
Async XLA Ops:
  7.2 3.4 copy-start
  7.2 3.4 copy-start.12
  7.2 4.1 copy-start.13
  7.2 3.3 copy-start.11
  7.2 2.1 copy-start.23
  7.2 99.1 %all-reduce.6.cloned.1.call-start = ((), (), s32[]{:S(2)}) async-start(), calls=%async_computation | async-start | bytes 1048576 | tf_op jit(solution)/shard_map/psum | solution.py:41
  8.6 4.1 copy-start.10
  11.3 1.4 copy-start.14
  12.7 188.5 %all-reduce.8.cloned.1.call-start = ((), (), s32[]{:S(2)}) async-start(), calls=%async_computation.1 | async-start | bytes 1048576 | tf_op jit(solution)/shard_map/psum | solution.py:55
  107.8 94.7 %copy-start.2 = (bf16[32,4096]{1,0:T(8,128)(2,1)}, bf16[32,4096]{1,0:T(8,128)(2,1)S(1)}, u32[]{:S(2)}) copy-start(bf16[32,4096]{1,0:T(8,128)(2,1)S(1)} %convert_element_type.55) | copy-start | bytes 786436
  109.8 188.4 %all-reduce.10.cloned.1.call-start = ((), (), s32[]{:S(2)}) async-start(), calls=%async_computation.2 | async-start | bytes 1048576 | tf_op jit(solution)/shard_map/psum | solution.py:55
  202.5 1.4 copy-start.15
  203.9 0.8 copy-start.1
  204.8 94.7 %copy-start.4 = (bf16[32,4096]{1,0:T(8,128)(2,1)}, bf16[32,4096]{1,0:T(8,128)(2,1)S(1)}, u32[]{:S(2)}) copy-start(bf16[32,4096]{1,0:T(8,128)(2,1)S(1)} %fusion.13) | copy-start | bytes 786436
  206.9 189.6 %all-reduce.12.cloned.1.call-start = ((), (), s32[]{:S(2)}) async-start(), calls=%async_computation.3 | async-start | bytes 1048576 | tf_op jit(solution)/shard_map/psum | solution.py:55
  299.6 3.6 copy-start.17
  301.1 2.0 copy-start.21
  303.9 96.8 %copy-start.9 = (f32[32,4096]{1,0:T(8,128)S(1)}, f32[32,4096]{1,0:T(8,128)}, u32[]{:S(2)}) copy-start(f32[32,4096]{1,0:T(8,128)} %get-tuple-element.6) | copy-start | bytes 1572868
  305.2 189.9 %all-reduce.14.cloned.1.call-start = ((), (), s32[]{:S(2)}) async-start(), calls=%async_computation.4 | async-start | bytes 1048576 | tf_op jit(solution)/shard_map/psum | solution.py:55
  396.5 4.1 copy-start.6
  400.0 0.7 copy-start.19
  400.9 0.7 copy-start.7
  402.3 1.4 copy-start.24
  402.4 92.7 %copy-start.8 = (bf16[32,4096]{1,0:T(8,128)(2,1)S(1)}, bf16[32,4096]{1,0:T(8,128)(2,1)}, u32[]{:S(2)}) copy-start(bf16[32,4096]{1,0:T(8,128)(2,1)} %copy-done.7) | copy-start | bytes 786436
  402.4 94.0 %copy-start.20 = (f32[32]{0:T(128)S(1)}, f32[32]{0:T(128)}, u32[]{:S(2)}) copy-start(f32[32]{0:T(128)} %copy-done.19) | copy-start | bytes 388
  402.4 94.0 %copy-start.3 = (bf16[32,4096]{1,0:T(8,128)(2,1)S(1)}, bf16[32,4096]{1,0:T(8,128)(2,1)}, u32[]{:S(2)}) copy-start(bf16[32,4096]{1,0:T(8,128)(2,1)} %copy-done.2) | copy-start | bytes 786436
  402.4 94.0 %copy-start.5 = (bf16[32,4096]{1,0:T(8,128)(2,1)S(1)}, bf16[32,4096]{1,0:T(8,128)(2,1)}, u32[]{:S(2)}) copy-start(bf16[32,4096]{1,0:T(8,128)(2,1)} %copy-done.4) | copy-start | bytes 786436
  402.4 94.0 %copy-start.16 = (f32[32]{0:T(128)S(1)}, f32[32]{0:T(128)}, u32[]{:S(2)}) copy-start(f32[32]{0:T(128)} %copy-done.15) | copy-start | bytes 388
  402.4 94.0 %copy-start.18 = (f32[32]{0:T(128)S(1)}, f32[32]{0:T(128)}, u32[]{:S(2)}) copy-start(f32[32]{0:T(128)} %copy-done.17) | copy-start | bytes 388
  403.7 126.5 %copy-start.22 = (f32[32]{0:T(128)S(1)}, f32[32]{0:T(128)}, u32[]{:S(2)}) copy-start(f32[32]{0:T(128)} %param.18) | copy-start | bytes 388
Sparse Core Ops, SparseCore 0:
  12.8 93.4 all-reduce.5
  110.0 91.1 all-reduce.7
  207.0 91.1 all-reduce.9
  305.3 91.1 all-reduce.11
  403.8 91.1 all-reduce.13
where the time goes:
time: 538 us; the launch traced here: 537 us
  waiting for transfers between devices  457 us (85%)
  blocking collectives  31.9 us (6%)
  other arithmetic  18.5 us (3%)
  between operations  15.5 us (3%)
  matrix products  10.1 us (2%)
    psum x4, waiting for transfers between devices, per_device(): local_sum = lax.psum(local_sum, 'ppl')  364 us
    psum x1, waiting for transfers between devices, per_device(): rhs = lax.psum(data_part, 'ppl') / noise_var + jnp.sqrt(ridge) * noise_coef  93.5 us
    psum x1, blocking collectives, per_device(): squares = lax.psum(jnp.sum(residual_new * residual_new, axis=1), 'ppl')  31.9 us
  transfers between devices with their start and end apart: 5, of which 5 were waited for; matrix products, arithmetic and copies ran while one was open for 0% of the time, Pallas kernels for 0%

commit v1 on v0

v1 whole, which is shorter than its diff:
```python
import functools

import jax
import jax.numpy as jnp
from jax import lax
from jax.experimental import pallas as pl
from jax.experimental.pallas import tpu as pltpu
from jax.sharding import PartitionSpec as P

ITERS = 4
PRIOR_DOF = 4.0
PRIOR_SCALE = 0.5
NT = (((1,), (1,)), ((), ()))
NN = (((1,), (0,)), ((), ()))
LANES = 128
F32 = jnp.float32
BF16 = jnp.bfloat16


def kernel(
    n,
    owners,
    block_ref,
    counts_ref,
    prior_ref,
    sigma_ref,
    gamma_ref,
    res_ref,
    noise_p_ref,
    noise_c_ref,
    coef_all_ref,
    geno_ref,
    coef_out,
    res_out,
    sigma_out,
    g,
    g_other,
    coef_v,
    noise_c,
    dir_low,
    dir_full,
    coef,
    search,
    t_send,
    t_recv,
    r_send,
    r_recv,
    x_send,
    x_recv,
    rs_send,
    rs_recv,
    first_send,
    first_recv,
    pd_send,
    pd_recv,
    ag_send,
    ag_recv,
    sc_send,
    sc_recv,
    f_recv,
    e_recv,
    ed_recv,
    loc_sem,
    pair_send,
    pair_recv,
    rs_ssem,
    rs_rsem,
    pd_ssem,
    pd_rsem,
    ag_ssem,
    ag_rsem,
    sc_ssem,
    sc_rsem,
    f_ssem,
    f_rsem,
):
    rows, batch = geno_ref.shape
    traits, width = coef_all_ref.shape
    half = batch // 2
    people = 2 * rows
    chips = n // 2
    chunk = half // owners
    first = (chips - owners) // 2
    me = lax.axis_index("ppl")
    chip = lax.div(me, 2)
    core = lax.rem(me, 2)
    mate = me + 1 - 2 * core
    mine = pl.multiple_of(core * half, LANES)
    theirs = pl.multiple_of((1 - core) * half, LANES)
    my_rows = pl.multiple_of(core * rows, rows)
    owner = jnp.logical_and(chip >= first, chip < first + owners)
    own = jnp.clip(chip - first, 0, owners - 1)
    own_col = pl.multiple_of(own * chunk, LANES)

    def remote(src, dst, send, recv, target):
        return pltpu.make_async_remote_copy(
            src_ref=src,
            dst_ref=dst,
            send_sem=send,
            recv_sem=recv,
            device_id={"ppl": target},
            device_id_type=pl.DeviceIdType.MESH,
        )

    load_coef = pltpu.make_async_copy(coef_all_ref, coef_v, loc_sem.at[0])
    load_mine = pltpu.make_async_copy(
        geno_ref.at[:, pl.ds(mine, half)], g.at[pl.ds(my_rows, rows), :], loc_sem.at[1]
    )
    load_other = pltpu.make_async_copy(geno_ref.at[:, pl.ds(theirs, half)], g_other, loc_sem.at[2])
    load_noise = pltpu.make_async_copy(
        noise_c_ref.at[:, pl.ds(pl.multiple_of(mine + own_col, LANES), chunk)], noise_c, loc_sem.at[3]
    )
    load_other.start()
    load_coef.start()
    load_mine.start()
    load_noise.start()

    barrier = pltpu.get_barrier_semaphore()

    @pl.loop(1, n)
    def _(step):
        pl.semaphore_signal(
            barrier,
            inc=1,
            device_id={"ppl": lax.rem(me + step, n)},
            device_id_type=pl.DeviceIdType.MESH,
        )

    row_id = lax.broadcasted_iota(jnp.int32, (traits, LANES), 0)
    lane_id = lax.broadcasted_iota(jnp.int32, (traits, LANES), 1)

    def to_row(column, kind):
        spread = jnp.where(lane_id == row_id + kind * traits, jnp.broadcast_to(column, (traits, LANES)), 0.0)
        return jnp.sum(spread, axis=0, keepdims=True)

    def to_col(row, kind):
        spread = jnp.where(lane_id == row_id + kind * traits, jnp.broadcast_to(row, (traits, LANES)), 0.0)
        return jnp.sum(spread, axis=1, keepdims=True)

    def small(ref):
        spread = jnp.where(
            lane_id[:, :traits] == row_id[:, :traits], jnp.broadcast_to(ref[...], (traits, traits)), 0.0
        )
        return jnp.sum(spread, axis=1, keepdims=True)

    noise_var = small(sigma_ref)
    ridge = small(prior_ref)

    def mask_of(device, size):
        return (lax.broadcasted_iota(jnp.int32, (1, size), 1) < counts_ref[device]).astype(F32)

    mask_own = mask_of(me, rows)
    mask = jnp.concatenate([mask_of(2 * chip, rows), mask_of(2 * chip + 1, rows)], axis=1)

    load_coef.wait()

    def old_part(offset):
        value = coef_v[:, pl.ds(offset, half)]
        for b in range(1, width // batch):
            value = jnp.where(
                block_ref[0] == b, coef_v[:, pl.ds(pl.multiple_of(offset + b * batch, LANES), half)], value
            )
        return value.astype(BF16)

    load_other.wait()
    pl.semaphore_wait(barrier, n - 1)
    g_copy = remote(g_other, g.at[pl.ds(my_rows, rows), :], pair_send.at[0], pair_recv.at[0], mate)
    g_copy.start()
    fitted_old = lax.dot_general(old_part(theirs), g_other[...], NT, preferred_element_type=F32)
    load_mine.wait()
    fitted_old = fitted_old + lax.dot_general(
        old_part(mine), g[pl.ds(my_rows, rows), :], NT, preferred_element_type=F32
    )
    partial = mask_own * (res_ref[...] + fitted_old)
    target = (mask_own * (partial + jnp.sqrt(noise_var) * noise_p_ref[...])).astype(BF16)
    t_send[...] = target
    r_send[...] = partial
    t_copy = remote(t_send, t_recv, pair_send.at[1], pair_recv.at[1], mate)
    r_copy = remote(r_send, r_recv, pair_send.at[2], pair_recv.at[2], mate)
    t_copy.start()
    r_copy.start()

    flip = jnp.where(chip < chips // 2, owners // 2, 0)

    def reduce_scatter(left, out, into):
        copies = []
        for i in range(owners):
            o = lax.rem(flip + i, owners)
            cols = pl.ds(pl.multiple_of(o * chunk, LANES), chunk)
            piece = lax.dot_general(left, g[:, cols], NN, preferred_element_type=F32)
            out[o] = piece.astype(out.dtype)
            copy = remote(
                out.at[o], into.at[chip], rs_ssem.at[o], rs_rsem.at[chip], 2 * (o + first) + core
            )

            @pl.when(o + first != chip)
            def _():
                copy.start()

            copies.append((o, copy))
        return copies

    def owner_sum(out, into):
        for k in range(chips):

            @pl.when(chip != k)
            def _():
                remote(out.at[0], into.at[k], rs_ssem.at[0], rs_rsem.at[k], me).wait_recv()

        into[chip] = out[own]
        total = into[0].astype(F32)
        for k in range(1, chips):
            total = total + into[k].astype(F32)
        return total

    def pd_copy(o, slot):
        return remote(
            pd_send.at[pl.ds(0, 1), :],
            pd_recv.at[slot, pl.ds(0, 1), :],
            pd_ssem.at[o],
            pd_rsem.at[slot],
            2 * (o + first) + core,
        )

    def send_pd(row):
        pd_send[0:1, :] = row
        for o in range(owners):

            @pl.when(o + first != chip)
            def _():
                pd_copy(o, chip).start()

    def owner_pd():
        for k in range(chips):

            @pl.when(chip != k)
            def _():
                pd_copy(0, k).wait_recv()

        pd_recv[chip, 0:1, :] = pd_send[0:1, :]
        total = pd_recv[0, 0:1, :]
        for k in range(1, chips):
            total = total + pd_recv[k, 0:1, :]
        return total

    def ag_copy(slot, k):
        return remote(ag_send, ag_recv.at[slot], ag_ssem.at[k], ag_rsem.at[slot], 2 * k + core)

    def sc_copy(slot, d):
        return remote(
            sc_send.at[pl.ds(0, 1), :], sc_recv.at[slot, pl.ds(0, 1), :], sc_ssem.at[d], sc_rsem.at[slot], d
        )

    def owner_gather(row):
        ag_send[...] = search[...].astype(BF16)
        sc_send[0:1, :] = row
        slot = 2 * own + core
        for i in range(chips):
            k = (i // 2 if i % 2 == 0 else chips - 1 - i // 2)

            @pl.when(chip != k)
            def _():
                ag_copy(own, k).start()

        for d in range(n):

            @pl.when(me != d)
            def _():
                sc_copy(slot, d).start()

        ag_recv[own] = ag_send[...]
        sc_recv[slot, 0:1, :] = row

    def finish(copies, with_pd):
        for o, copy in copies:

            @pl.when(o + first != chip)
            def _():
                copy.wait_send()

        if with_pd:
            for o in range(owners):

                @pl.when(o + first != chip)
                def _():
                    pd_copy(o, chip).wait_send()

        @pl.when(owner)
        def _():
            for k in range(chips):

                @pl.when(chip != k)
                def _():
                    ag_copy(own, k).wait_send()

            for d in range(n):

                @pl.when(me != d)
                def _():
                    sc_copy(2 * own + core, d).wait_send()

    def wait_gather():
        for o in range(owners):
            for c in range(2):

                @pl.when(jnp.logical_or(o + first != chip, c != core))
                def _():
                    sc_copy(2 * o + c, 0).wait_recv()

        for o in range(owners):

            @pl.when(o + first != chip)
            def _():
                ag_copy(o, 0).wait_recv()

        total = sc_recv[0, 0:1, :]
        for s in range(1, 2 * owners):
            total = total + sc_recv[s, 0:1, :]
        return total, sc_recv[0, 0:1, :]

    t_copy.wait()
    g_copy.wait()
    targets = jnp.concatenate(
        [
            jnp.where(core == 0, target, t_recv[...]),
            jnp.where(core == 0, t_recv[...], target),
        ],
        axis=1,
    )
    copies = reduce_scatter(targets, first_send, first_recv)

    load_noise.wait()

    @pl.when(owner)
    def _():
        rhs = owner_sum(first_send, first_recv) / noise_var + jnp.sqrt(ridge) * noise_c[...]
        search[...] = rhs
        owner_gather(to_row(jnp.sum(rhs * rhs, axis=1, keepdims=True), 0))

    r_copy.wait()
    residual = jnp.concatenate(
        [
            jnp.where(core == 0, partial, r_recv[...]),
            jnp.where(core == 0, r_recv[...], partial),
        ],
        axis=1,
    )
    totals, _unused = wait_gather()
    norm = to_col(totals, 0)
    for o in range(owners):
        dir_low[:, o * chunk : (o + 1) * chunk] = ag_recv[o]
        dir_full[:, o * chunk : (o + 1) * chunk] = ag_recv[o].astype(F32)
    coef[...] = jnp.zeros_like(coef)
    finish(copies, False)

    for number in range(ITERS):
        last = number == ITERS - 1
        low = dir_low[...]
        wide = low.astype(F32)
        image_part = lax.dot_general(low, g[...], NT, preferred_element_type=F32)
        sq_part = jnp.sum(wide * wide, axis=1, keepdims=True)
        x_send[:, :people] = image_part
        x_send[:, people:] = jnp.broadcast_to(sq_part, (traits, LANES))
        x_copy = remote(x_send, x_recv, pair_send.at[1], pair_recv.at[1], mate)
        x_copy.start()
        if last:
            e_copy = remote(coef, e_recv, pair_send.at[2], pair_recv.at[2], mate)
            d_copy = remote(dir_low, ed_recv, pair_send.at[3], pair_recv.at[3], mate)
            e_copy.start()
            d_copy.start()
        x_copy.wait()
        image = mask * (image_part + x_recv[:, :people])
        dir_sq = sq_part + x_recv[:, people : people + 1]
        image_low = image.astype(BF16)
        dot_row = to_row(jnp.sum(image_low.astype(F32) * image, axis=1, keepdims=True), 0)
        if not last:
            send_pd(dot_row)
            copies = reduce_scatter(image_low, rs_send, rs_recv)

            @pl.when(owner)
            def _():
                pd = to_col(owner_pd(), 0)
                step = norm / (pd / noise_var + ridge * dir_sq)
                applied = owner_sum(rs_send, rs_recv) / noise_var + ridge * dir_low[:, pl.ds(own_col, chunk)].astype(F32)
                fresh = search[...] - step * applied
                search[...] = fresh
                owner_gather(to_row(jnp.sum(fresh * fresh, axis=1, keepdims=True), 0) + to_row(step, 1))

            totals, head = wait_gather()
            norm_next = to_col(totals, 0)
            step = to_col(head, 1)
            ratio = norm_next / norm
            norm = norm_next
            coef[...] += step * wide
            residual = residual - step * image
            for o in range(owners):
                cols = slice(o * chunk, (o + 1) * chunk)
                fresh = ag_recv[o].astype(F32) + ratio * dir_full[:, cols]
                dir_full[:, cols] = fresh
                dir_low[:, cols] = fresh.astype(BF16)
            finish(copies, True)

    row = (
        dot_row
        + to_row(jnp.sum(residual * image, axis=1, keepdims=True), 1)
        + to_row(jnp.sum(residual * residual, axis=1, keepdims=True), 2)
        + to_row(jnp.sum(image * image, axis=1, keepdims=True), 3)
    )
    pd_send[0:1, :] = row

    def f_copy(slot, k):
        return remote(
            pd_send.at[pl.ds(0, 1), :], f_recv.at[slot, pl.ds(0, 1), :], f_ssem.at[k], f_rsem.at[slot], 2 * k + core
        )

    for k in range(chips):

        @pl.when(chip != k)
        def _():
            f_copy(chip, k).start()

    f_recv[chip, 0:1, :] = row
    e_copy.wait()
    d_copy.wait()
    for k in range(chips):

        @pl.when(chip != k)
        def _():
            f_copy(k, 0).wait_recv()

    total = f_recv[0, 0:1, :]
    for k in range(1, chips):
        total = total + f_recv[k, 0:1, :]
    step = norm / (to_col(total, 0) / noise_var + ridge * dir_sq)
    squares = to_col(total, 2) - 2.0 * step * to_col(total, 1) + step * step * to_col(total, 3)
    residual_new = residual - step * image
    res_out[...] = jnp.where(core == 0, residual_new[:, :rows], residual_new[:, rows:])
    present = counts_ref[0]
    for d in range(1, n):
        present = present + counts_ref[d]
    sigma = (squares + PRIOR_DOF * PRIOR_SCALE) / ((present.astype(F32) + PRIOR_DOF) * small(gamma_ref))
    sigma_out[...] = to_row(sigma, 0)
    coef_out[:, pl.ds(mine, half)] = coef[...] + step * wide
    coef_out[:, pl.ds(theirs, half)] = e_recv[...] + step * ed_recv[...].astype(F32)
    for k in range(chips):

        @pl.when(chip != k)
        def _():
            f_copy(chip, k).wait_send()


def per_device(
    n,
    genotypes,
    residual,
    noise_people,
    noise_coef,
    coef_all,
    block_index,
    prior_prec,
    sigma2_old,
    gamma_draw,
    valid_counts,
):
    rows, batch = genotypes.shape
    traits, width = coef_all.shape
    half = batch // 2
    people = 2 * rows
    chips = n // 2
    owners = max(1, min(chips // 2, half // LANES))
    chunk = half // owners
    vmem = pl.BlockSpec(memory_space=pltpu.VMEM)
    smem = pl.BlockSpec(memory_space=pltpu.SMEM)
    hbm = pl.BlockSpec(memory_space=pl.ANY)
    dma = pltpu.SemaphoreType.DMA
    batch_coef, residual_new, sigma = pl.pallas_call(
        functools.partial(kernel, n, owners),
        out_shape=(
            jax.ShapeDtypeStruct((traits, batch), F32),
            jax.ShapeDtypeStruct((traits, rows), F32),
            jax.ShapeDtypeStruct((1, LANES), F32),
        ),
        in_specs=[smem, smem, vmem, vmem, vmem, vmem, vmem, hbm, hbm, hbm],
        out_specs=(vmem, vmem, vmem),
        scratch_shapes=[
            pltpu.VMEM((people, half), BF16),
            pltpu.VMEM((rows, half), BF16),
            pltpu.VMEM((traits, width), F32),
            pltpu.VMEM((traits, chunk), F32),
            pltpu.VMEM((traits, half), BF16),
            pltpu.VMEM((traits, half), F32),
            pltpu.VMEM((traits, half), F32),
            pltpu.VMEM((traits, chunk), F32),
            pltpu.VMEM((traits, rows), BF16),
            pltpu.VMEM((traits, rows), BF16),
            pltpu.VMEM((traits, rows), F32),
            pltpu.VMEM((traits, rows), F32),
            pltpu.VMEM((traits, people + LANES), F32),
            pltpu.VMEM((traits, people + LANES), F32),
            pltpu.VMEM((owners, traits, chunk), BF16),
            pltpu.VMEM((chips, traits, chunk), BF16),
            pltpu.VMEM((owners, traits, chunk), F32),
            pltpu.VMEM((chips, traits, chunk), F32),
            pltpu.VMEM((8, LANES), F32),
            pltpu.VMEM((chips, 8, LANES), F32),
            pltpu.VMEM((traits, chunk), BF16),
            pltpu.VMEM((owners, traits, chunk), BF16),
            pltpu.VMEM((8, LANES), F32),
            pltpu.VMEM((2 * owners, 8, LANES), F32),
            pltpu.VMEM((chips, 8, LANES), F32),
            pltpu.VMEM((traits, half), F32),
            pltpu.VMEM((traits, half), BF16),
            dma((4,)),
            dma((4,)),
            dma((4,)),
            dma((owners,)),
            dma((chips,)),
            dma((owners,)),
            dma((chips,)),
            dma((chips,)),
            dma((owners,)),
            dma((n,)),
            dma((2 * owners,)),
            dma((chips,)),
            dma((chips,)),
        ],
        compiler_params=pltpu.CompilerParams(
            collective_id=0, has_side_effects=True, vmem_limit_bytes=40 * 1024 * 1024
        ),
    )(
        block_index,
        valid_counts,
        prior_prec[None, :],
        sigma2_old[None, :],
        gamma_draw[None, :],
        residual,
        noise_people,
        noise_coef,
        coef_all,
        genotypes,
    )
    coef_new = lax.dynamic_update_slice_in_dim(coef_all, batch_coef, block_index[0] * batch, 1)
    return (coef_new, residual_new, sigma[0, :traits])


def solution(mesh):
    return jax.shard_map(
        functools.partial(per_device, mesh.shape["ppl"]),
        mesh=mesh,
        in_specs=(
            P(("trait", "ppl"), None),
            P("trait", "ppl"),
            P("trait", "ppl"),
            P("trait", None),
            P("trait", None),
            P("trait"),
            P("trait"),
            P("trait"),
            P("trait"),
            P("trait"),
        ),
        out_specs=(P("trait", None), P("trait", "ppl"), P("trait")),
        check_vma=False,
    )
```

time: 538 us -> 76.8 us (0.14)
  waiting for transfers between devices: 457 us -> 0 us
  Pallas kernels: 0 us -> 69.9 us
  blocking collectives: 31.9 us -> 0 us
  other arithmetic: 18.5 us -> 0 us
  between operations: 15.5 us -> 1.4 us
  matrix products: 10.1 us -> 0 us
    psum x5 -> x0, waiting for transfers between devices: 457 us -> none  [the longest x4 364 us: per_device(): local_sum = lax.psum(local_sum, 'ppl')]
    pallas_call x0 -> x1, Pallas kernels: none -> 69.9 us  [per_device(): pl.pallas_call(functools.partial(kernel, n, owners), out_shape=(jax.Shape...]
    psum x1 -> x0, blocking collectives: 31.9 us -> none  [per_device(): squares = lax.psum(jnp.sum(residual_new * residual_new, axis=1), 'ppl')]
    reduce_sum x10 -> x0, other arithmetic: 12.5 us -> none  [the longest x4 5.41 us: per_device(): step_size = norm_now / jnp.sum(dir_full * applied, axis=1)]
    dot_general x10 -> x0, matrix products: 10.1 us -> none  [the longest x4 5.14 us: per_device(): jnp.dot(image.astype(jnp.bfloat16), genotypes, preferred_element_type=jnp...]
  transfers between devices with their start and end apart: 5 -> 0, of which waited for: 5 -> 0; matrix products, arithmetic and copies ran while one was open for 0% -> 0% of each run, Pallas kernels for 0% -> 0%
where the time goes in v1:
time: 76.8 us; the launch traced here: 76.5 us
  Pallas kernels  69.9 us (91%)
  local copies, waits for them, and re-layouts  5.16 us (7%)
  between operations  1.4 us (2%)
    pallas_call x1, Pallas kernels, per_device(): pl.pallas_call(functools.partial(kernel, n, owners), out_shape=(jax.Shape...  69.9 us
    unnamed x20, local copies, waits for them, and re-layouts  4.56 us

profile of v1, /device:TPU:0, one launch (start us, length us, event | category | flops | bytes accessed | tf_op | source)
XLA Modules:
  0.0 76.5 jit_solution(5621255646002259996)
XLA Ops:
  0.6 0.0 copy-start.1
  0.6 0.0 copy-start.6
  0.7 0.0 copy-start.7
  0.7 0.0 copy-start.8
  0.7 0.0 copy-start.5
  0.7 1.4 %copy.17.coef_all_ref = f32[32,8192]{1,0:T(8,128)S(1)} copy(f32[32,8192]{1,0:T(8,128)} %param.14) | data formatting | bytes 2097152
  2.7 0.0 copy-done.1
  2.7 0.0 copy-done.6
  2.7 0.0 copy-done.7
  2.7 0.0 copy-done.8
  2.7 0.0 copy-done.5
  2.8 0.0 copy-start.2
  2.8 1.0 %copy-done.2 = f32[32,4096]{1,0:T(8,128)S(1)} copy-done((f32[32,4096]{1,0:T(8,128)S(1)}, f32[32,4096]{1,0:T(8,128)}, u32[]{:S(2)}) %copy-start.2) | copy-done | bytes 524312
  3.8 0.0 copy-start.3
  3.8 0.8 copy-done.3
  4.6 0.0 copy-start.4
  4.6 0.8 copy-done.4
  5.3 69.9 %shard_map.121 = (f32[32,4096]{1,0:T(8,128)S(1)}, f32[32,256]{1,0:T(8,128)S(1)}, f32[1,128]{1,0:T(1,128)S(1)}) custom-call(s32[1]{0:T(128)S(6)} %copy.16.block_ref, s32[16]{0:T(128)S(1)} %copy-done.5, f32[1,32]{1,0:T(1,128)S(1)} %bitcast.6, f32[1,32]{1,0:T(1,128)S(1)} %bitcast.7, f32[1,32]{1,0:T(1,128)S(1)} %bitcast.8, f32[32,256]{1,0:T(8,128)S(1)} %copy-done.3, ...), custom_call_target="tpu_custom_call" | custom-call | tf_op jit(solution)/shard_map/pallas_call | solution.py:476
  75.3 0.0 copy-start
  75.3 0.6 slice_bitcast_fusion
  75.9 0.6 copy.18
  76.5 0.0 copy-done
  (1 shorter events, 0.0 us)
Async XLA Ops:
  0.6 2.1 %copy-start.1 = (bf16[256,4096]{1,0:T(8,128)(2,1)S(1)}, bf16[256,4096]{1,0:T(8,128)(2,1)}, u32[]{:S(2)}) copy-start(bf16[256,4096]{1,0:T(8,128)(2,1)} %geno_ref.1) | copy-start | bytes 6291460
  0.6 2.1 %copy-start.6 = (f32[32]{0:T(128)S(1)}, f32[32]{0:T(128)}, u32[]{:S(2)}) copy-start(f32[32]{0:T(128)} %param.16) | copy-start | bytes 388
  0.7 2.1 %copy-start.7 = (f32[32]{0:T(128)S(1)}, f32[32]{0:T(128)}, u32[]{:S(2)}) copy-start(f32[32]{0:T(128)} %param.17) | copy-start | bytes 388
  0.7 2.1 %copy-start.8 = (f32[32]{0:T(128)S(1)}, f32[32]{0:T(128)}, u32[]{:S(2)}) copy-start(f32[32]{0:T(128)} %param.18) | copy-start | bytes 388
  0.7 2.1 %copy-start.5 = (s32[16]{0:T(128)S(1)}, s32[16]{0:T(128)}, u32[]{:S(2)}) copy-start(s32[16]{0:T(128)} %counts_ref.1) | copy-start | bytes 196
  2.8 1.0 %copy-start.2 = (f32[32,4096]{1,0:T(8,128)S(1)}, f32[32,4096]{1,0:T(8,128)}, u32[]{:S(2)}) copy-start(f32[32,4096]{1,0:T(8,128)} %noise_c_ref.1) | copy-start | bytes 1572868
  3.8 0.8 copy-start.3
  4.6 0.8 copy-start.4
  75.3 1.2 %copy-start = (f32[32,8192]{1,0:T(8,128)}, f32[32,8192]{1,0:T(8,128)S(1)}, u32[]{:S(2)}) copy-start(f32[32,8192]{1,0:T(8,128)S(1)} %constant_dynamic-update-slice_fusion) | copy-start | bytes 3145732

commit v2 on v1

--- a/solution.py
+++ b/solution.py
@@ -13,6 +13,7 @@
 NT = (((1,), (1,)), ((), ()))
 NN = (((1,), (0,)), ((), ()))
 LANES = 128
+CODE_MAX = 32767.0
 F32 = jnp.float32
 BF16 = jnp.bfloat16
 
@@ -20,6 +21,19 @@
 def kernel(
     n,
     owners,
+    block_hbm,
+    counts_hbm,
+    prior_hbm,
+    sigma_hbm,
+    gamma_hbm,
+    res_hbm,
+    noise_p_hbm,
+    noise_c_ref,
+    coef_all_ref,
+    geno_ref,
+    coef_out,
+    res_out,
+    sigma_out,
     block_ref,
     counts_ref,
     prior_ref,
@@ -27,12 +41,6 @@
     gamma_ref,
     res_ref,
     noise_p_ref,
-    noise_c_ref,
-    coef_all_ref,
-    geno_ref,
-    coef_out,
-    res_out,
-    sigma_out,
     g,
     g_other,
     coef_v,
@@ -51,6 +59,7 @@
     rs_recv,
     first_send,
     first_recv,
+    scale_send,
     pd_send,
     pd_recv,
     ag_send,
@@ -110,11 +119,20 @@
     load_noise = pltpu.make_async_copy(
         noise_c_ref.at[:, pl.ds(pl.multiple_of(mine + own_col, LANES), chunk)], noise_c, loc_sem.at[3]
     )
-    load_other.start()
-    load_coef.start()
-    load_mine.start()
-    load_noise.start()
-
+    small_loads = [
+        pltpu.make_async_copy(src, dst, loc_sem.at[4 + i])
+        for i, (src, dst) in enumerate(
+            (
+                (counts_hbm, counts_ref),
+                (block_hbm, block_ref),
+                (prior_hbm, prior_ref),
+                (sigma_hbm, sigma_ref),
+                (gamma_hbm, gamma_ref),
+                (res_hbm, res_ref),
+                (noise_p_hbm, noise_p_ref),
+            )
+        )
+    ]
     barrier = pltpu.get_barrier_semaphore()
 
     @pl.loop(1, n)
@@ -126,6 +144,13 @@
             device_id_type=pl.DeviceIdType.MESH,
         )
 
+    load_other.start()
+    load_coef.start()
+    for load in small_loads:
+        load.start()
+    load_mine.start()
+    load_noise.start()
+
     row_id = lax.broadcasted_iota(jnp.int32, (traits, LANES), 0)
     lane_id = lax.broadcasted_iota(jnp.int32, (traits, LANES), 1)
 
@@ -142,6 +167,9 @@
             lane_id[:, :traits] == row_id[:, :traits], jnp.broadcast_to(ref[...], (traits, traits)), 0.0
         )
         return jnp.sum(spread, axis=1, keepdims=True)
+
+    for load in small_loads:
+        load.wait()
 
     noise_var = small(sigma_ref)
     ridge = small(prior_ref)
@@ -163,10 +191,10 @@
         return value.astype(BF16)
 
     load_other.wait()
+    fitted_old = lax.dot_general(old_part(theirs), g_other[...], NT, preferred_element_type=F32)
     pl.semaphore_wait(barrier, n - 1)
     g_copy = remote(g_other, g.at[pl.ds(my_rows, rows), :], pair_send.at[0], pair_recv.at[0], mate)
     g_copy.start()
-    fitted_old = lax.dot_general(old_part(theirs), g_other[...], NT, preferred_element_type=F32)
     load_mine.wait()
     fitted_old = fitted_old + lax.dot_general(
         old_part(mine), g[pl.ds(my_rows, rows), :], NT, preferred_element_type=F32
@@ -182,13 +210,33 @@
 
     flip = jnp.where(chip < chips // 2, owners // 2, 0)
 
-    def reduce_scatter(left, out, into):
+    def scale_copy(o, slot):
+        return remote(
+            scale_send.at[o, pl.ds(0, 1), :],
+            pd_recv.at[slot, pl.ds(0, 1), :],
+            pd_ssem.at[o],
+            pd_rsem.at[slot],
+            2 * (o + first) + core,
+        )
+
+    def reduce_scatter(left, out, into, coded):
         copies = []
         for i in range(owners):
             o = lax.rem(flip + i, owners)
             cols = pl.ds(pl.multiple_of(o * chunk, LANES), chunk)
             piece = lax.dot_general(left, g[:, cols], NN, preferred_element_type=F32)
-            out[o] = piece.astype(out.dtype)
+            if coded:
+                peak = jnp.max(jnp.abs(piece), axis=1, keepdims=True)
+                gain = jnp.where(peak > 1e-30, CODE_MAX / jnp.maximum(peak, 1e-30), 0.0)
+                out[o] = jnp.round(piece * gain).astype(jnp.int32).astype(out.dtype)
+                scale_send[o, 0:1, :] = to_row(peak * (1.0 / CODE_MAX), 0)
+
+                @pl.when(o + first != chip)
+                def _():
+                    scale_copy(o, chip).start()
+
+            else:
+                out[o] = piece.astype(out.dtype)
             copy = remote(
                 out.at[o], into.at[chip], rs_ssem.at[o], rs_rsem.at[chip], 2 * (o + first) + core
             )
@@ -200,17 +248,27 @@
             copies.append((o, copy))
         return copies
 
-    def owner_sum(out, into):
+    def owner_sum(out, into, coded):
         for k in range(chips):
 
             @pl.when(chip != k)
             def _():
                 remote(out.at[0], into.at[k], rs_ssem.at[0], rs_rsem.at[k], me).wait_recv()
+                if coded:
+                    scale_copy(0, k).wait_recv()
 
         into[chip] = out[own]
-        total = into[0].astype(F32)
+        if coded:
+            pd_recv[chip, 0:1, :] = scale_send[own, 0:1, :]
+
+        def term(k):
+            if coded:
+                return into[k].astype(jnp.int32).astype(F32) * to_col(pd_recv[k, 0:1, :], 0)
+            return into[k].astype(F32)
+
+        total = term(0)
         for k in range(1, chips):
-            total = total + into[k].astype(F32)
+            total = total + term(k)
         return total
 
     def pd_copy(o, slot):
@@ -271,19 +329,18 @@
         ag_recv[own] = ag_send[...]
         sc_recv[slot, 0:1, :] = row
 
-    def finish(copies, with_pd):
+    def finish(copies, row_copy):
         for o, copy in copies:
 
             @pl.when(o + first != chip)
             def _():
                 copy.wait_send()
 
-        if with_pd:
-            for o in range(owners):
-
-                @pl.when(o + first != chip)
-                def _():
-                    pd_copy(o, chip).wait_send()
+        for o in range(owners):
+
+            @pl.when(o + first != chip)
+            def _():
+                row_copy(o, chip).wait_send()
 
         @pl.when(owner)
         def _():
@@ -327,13 +384,13 @@
         ],
         axis=1,
     )
-    copies = reduce_scatter(targets, first_send, first_recv)
+    copies = reduce_scatter(targets, first_send, first_recv, True)
 
     load_noise.wait()
 
     @pl.when(owner)
     def _():
-        rhs = owner_sum(first_send, first_recv) / noise_var + jnp.sqrt(ridge) * noise_c[...]
+        rhs = owner_sum(first_send, first_recv, True) / noise_var + jnp.sqrt(ridge) * noise_c[...]
         search[...] = rhs
         owner_gather(to_row(jnp.sum(rhs * rhs, axis=1, keepdims=True), 0))
 
@@ -351,7 +408,7 @@
         dir_low[:, o * chunk : (o + 1) * chunk] = ag_recv[o]
         dir_full[:, o * chunk : (o + 1) * chunk] = ag_recv[o].astype(F32)
     coef[...] = jnp.zeros_like(coef)
-    finish(copies, False)
+    finish(copies, scale_copy)
 
     for number in range(ITERS):
         last = number == ITERS - 1
@@ -375,13 +432,13 @@
         dot_row = to_row(jnp.sum(image_low.astype(F32) * image, axis=1, keepdims=True), 0)
         if not last:
             send_pd(dot_row)
-            copies = reduce_scatter(image_low, rs_send, rs_recv)
+            copies = reduce_scatter(image_low, rs_send, rs_recv, False)
 
             @pl.when(owner)
             def _():
                 pd = to_col(owner_pd(), 0)
                 step = norm / (pd / noise_var + ridge * dir_sq)
-                applied = owner_sum(rs_send, rs_recv) / noise_var + ridge * dir_low[:, pl.ds(own_col, chunk)].astype(F32)
+                applied = owner_sum(rs_send, rs_recv, False) / noise_var + ridge * dir_low[:, pl.ds(own_col, chunk)].astype(F32)
                 fresh = search[...] - step * applied
                 search[...] = fresh
                 owner_gather(to_row(jnp.sum(fresh * fresh, axis=1, keepdims=True), 0) + to_row(step, 1))
@@ -398,7 +455,7 @@
                 fresh = ag_recv[o].astype(F32) + ratio * dir_full[:, cols]
                 dir_full[:, cols] = fresh
                 dir_low[:, cols] = fresh.astype(BF16)
-            finish(copies, True)
+            finish(copies, pd_copy)
 
     row = (
         dot_row
@@ -439,9 +496,13 @@
     for d in range(1, n):
         present = present + counts_ref[d]
     sigma = (squares + PRIOR_DOF * PRIOR_SCALE) / ((present.astype(F32) + PRIOR_DOF) * small(gamma_ref))
-    sigma_out[...] = to_row(sigma, 0)
-    coef_out[:, pl.ds(mine, half)] = coef[...] + step * wide
-    coef_out[:, pl.ds(theirs, half)] = e_recv[...] + step * ed_recv[...].astype(F32)
+    sigma_out[...] = to_row(sigma, 0)[:, :traits]
+    new_mine = coef[...] + step * wide
+    new_theirs = e_recv[...] + step * ed_recv[...].astype(F32)
+    for b in range(width // batch):
+        for offset, value in ((mine, new_mine), (theirs, new_theirs)):
+            cols = pl.ds(pl.multiple_of(offset + b * batch, LANES), half)
+            coef_out[:, cols] = jnp.where(block_ref[0] == b, value, coef_v[:, cols])
     for k in range(chips):
 
         @pl.when(chip != k)
@@ -470,19 +531,25 @@
     owners = max(1, min(chips // 2, half // LANES))
     chunk = half // owners
     vmem = pl.BlockSpec(memory_space=pltpu.VMEM)
-    smem = pl.BlockSpec(memory_space=pltpu.SMEM)
-    hbm = pl.BlockSpec(memory_space=pl.ANY)
+    hbm = pl.BlockSpec(memory_space=pltpu.HBM)
     dma = pltpu.SemaphoreType.DMA
-    batch_coef, residual_new, sigma = pl.pallas_call(
+    coef_new, residual_new, sigma = pl.pallas_call(
         functools.partial(kernel, n, owners),
         out_shape=(
-            jax.ShapeDtypeStruct((traits, batch), F32),
+            jax.ShapeDtypeStruct((traits, width), F32),
             jax.ShapeDtypeStruct((traits, rows), F32),
-            jax.ShapeDtypeStruct((1, LANES), F32),
+            jax.ShapeDtypeStruct((1, traits), F32),
         ),
-        in_specs=[smem, smem, vmem, vmem, vmem, vmem, vmem, hbm, hbm, hbm],
+        in_specs=[hbm] * 10,
         out_specs=(vmem, vmem, vmem),
         scratch_shapes=[
+            pltpu.SMEM(block_index.shape, jnp.int32),
+            pltpu.SMEM(valid_counts.shape, jnp.int32),
+            pltpu.VMEM((1, traits), F32),
+            pltpu.VMEM((1, traits), F32),
+            pltpu.VMEM((1, traits), F32),
+            pltpu.VMEM((traits, rows), F32),
+            pltpu.VMEM((traits, rows), F32),
             pltpu.VMEM((people, half), BF16),
             pltpu.VMEM((rows, half), BF16),
             pltpu.VMEM((traits, width), F32),
@@ -499,8 +566,9 @@
             pltpu.VMEM((traits, people + LANES), F32),
             pltpu.VMEM((owners, traits, chunk), BF16),
             pltpu.VMEM((chips, traits, chunk), BF16),
-            pltpu.VMEM((owners, traits, chunk), F32),
-            pltpu.VMEM((chips, traits, chunk), F32),
+            pltpu.VMEM((owners, traits, chunk), jnp.int16),
+            pltpu.VMEM((chips, traits, chunk), jnp.int16),
+            pltpu.VMEM((owners, 8, LANES), F32),
             pltpu.VMEM((8, LANES), F32),
             pltpu.VMEM((chips, 8, LANES), F32),
             pltpu.VMEM((traits, chunk), BF16),
@@ -510,7 +578,7 @@
             pltpu.VMEM((chips, 8, LANES), F32),
             pltpu.VMEM((traits, half), F32),
             pltpu.VMEM((traits, half), BF16),
-            dma((4,)),
+            dma((11,)),
             dma((4,)),
             dma((4,)),
             dma((owners,)),
@@ -525,7 +593,7 @@
             dma((chips,)),
         ],
         compiler_params=pltpu.CompilerParams(
-            collective_id=0, has_side_effects=True, vmem_limit_bytes=40 * 1024 * 1024
+            collective_id=0, has_side_effects=True, vmem_limit_bytes=60 * 1024 * 1024
         ),
     )(
         block_index,
@@ -539,8 +607,7 @@
         coef_all,
         genotypes,
     )
-    coef_new = lax.dynamic_update_slice_in_dim(coef_all, batch_coef, block_index[0] * batch, 1)
-    return (coef_new, residual_new, sigma[0, :traits])
+    return (coef_new, residual_new, sigma.reshape(traits))
 
 
 def solution(mesh):

time: 76.8 us -> 72.1 us (0.939)
  Pallas kernels: 69.9 us -> 67.3 us
  local copies, waits for them, and re-layouts: 5.16 us -> 3.4 us
    pallas_call x1, Pallas kernels: 69.9 us -> 67.3 us  [per_device(): pl.pallas_call(functools.partial(kernel, n, owners), out_shape=(jax.Shape...]
    unnamed x20 -> x7, local copies, waits for them, and re-layouts: 4.56 us -> 3.4 us
where the time goes in v2:
time: 72.1 us; the launch traced here: 72 us
  Pallas kernels  67.3 us (93%)
  local copies, waits for them, and re-layouts  3.4 us (5%)
  between operations  1.3 us (2%)
    pallas_call x1, Pallas kernels, per_device(): pl.pallas_call(functools.partial(kernel, n, owners), out_shape=(jax.Shape...  67.3 us
    unnamed x7, local copies, waits for them, and re-layouts  3.4 us

profile of v2, /device:TPU:0, one launch (start us, length us, event | category | flops | bytes accessed | tf_op | source)
XLA Modules:
  0.0 72.0 jit_solution(6232986274331299914)
XLA Ops:
  1.3 67.3 %shard_map.121 = (f32[32,8192]{1,0:T(8,128)}, f32[32,256]{1,0:T(8,128)}, f32[1,32]{1,0:T(1,128)}) custom-call(s32[1]{0:T(128)S(6)} %copy.16.block_hbm, s32[16]{0:T(128)} %counts_hbm.1, f32[1,32]{1,0:T(1,128)} %bitcast.4, f32[1,32]{1,0:T(1,128)} %bitcast.5, f32[1,32]{1,0:T(1,128)} %bitcast.6, f32[32,256]{1,0:T(8,128)} %res_hbm.1, f32[32,256]{1,0:T(8,128)} %noise_p_hbm.1, ...), custom_call_target="tpu_custom_call" | custom-call | tf_op jit(solution)/shard_map/pallas_call | solution.py:536
  68.5 0.0 copy-start
  68.6 0.0 copy-start.1
  68.6 2.3 %copy.17 = f32[32,8192]{1,0:T(8,128)} copy(f32[32,8192]{1,0:T(8,128)} %get-tuple-element.12) | data formatting | bytes 2097152
  70.8 0.0 copy-done
  70.8 0.6 copy.18
  71.4 0.0 copy-done.1
  71.4 0.5 copy.19
Async XLA Ops:
  68.5 2.3 %copy-start = (f32[32,256]{1,0:T(8,128)S(1)}, f32[32,256]{1,0:T(8,128)}, u32[]{:S(2)}) copy-start(f32[32,256]{1,0:T(8,128)} %get-tuple-element.13) | copy-start | bytes 98308
  68.6 2.9 %copy-start.1 = (f32[1,32]{1,0:T(1,128)S(1)}, f32[1,32]{1,0:T(1,128)}, u32[]{:S(2)}) copy-start(f32[1,32]{1,0:T(1,128)} %get-tuple-element.8) | copy-start | bytes 388

commit v3 on v2

--- a/solution.py
+++ b/solution.py
@@ -528,7 +528,7 @@
     half = batch // 2
     people = 2 * rows
     chips = n // 2
-    owners = max(1, min(chips // 2, half // LANES))
+    owners = max(1, min(chips, half // LANES))
     chunk = half // owners
     vmem = pl.BlockSpec(memory_space=pltpu.VMEM)
     hbm = pl.BlockSpec(memory_space=pltpu.HBM)

time: 72.1 us -> 71.5 us (level)
  no operation moved by 1% of the time
where the time goes in v3:
time: 71.5 us; the launch traced here: 71.3 us
  Pallas kernels  66.6 us (93%)
  local copies, waits for them, and re-layouts  3.4 us (5%)
  between operations  1.3 us (2%)
    pallas_call x1, Pallas kernels, per_device(): pl.pallas_call(functools.partial(kernel, n, owners), out_shape=(jax.Shape...  66.6 us
    unnamed x7, local copies, waits for them, and re-layouts  3.4 us

profile of v3, /device:TPU:0, one launch (start us, length us, event | category | flops | bytes accessed | tf_op | source)
XLA Modules:
  0.0 71.3 jit_solution(8545630912315230865)
XLA Ops:
  1.3 66.6 %shard_map.121 = (f32[32,8192]{1,0:T(8,128)}, f32[32,256]{1,0:T(8,128)}, f32[1,32]{1,0:T(1,128)}) custom-call(s32[1]{0:T(128)S(6)} %copy.16.block_hbm, s32[16]{0:T(128)} %counts_hbm.1, f32[1,32]{1,0:T(1,128)} %bitcast.4, f32[1,32]{1,0:T(1,128)} %bitcast.5, f32[1,32]{1,0:T(1,128)} %bitcast.6, f32[32,256]{1,0:T(8,128)} %res_hbm.1, f32[32,256]{1,0:T(8,128)} %noise_p_hbm.1, ...), custom_call_target="tpu_custom_call" | custom-call | tf_op jit(solution)/shard_map/pallas_call | solution.py:536
  67.9 0.0 copy-start
  67.9 0.0 copy-start.1
  67.9 2.3 %copy.17 = f32[32,8192]{1,0:T(8,128)} copy(f32[32,8192]{1,0:T(8,128)} %get-tuple-element.12) | data formatting | bytes 2097152
  70.2 0.0 copy-done
  70.2 0.6 copy.18
  70.8 0.0 copy-done.1
  70.8 0.5 copy.19
Async XLA Ops:
  67.9 2.3 %copy-start = (f32[32,256]{1,0:T(8,128)S(1)}, f32[32,256]{1,0:T(8,128)}, u32[]{:S(2)}) copy-start(f32[32,256]{1,0:T(8,128)} %get-tuple-element.13) | copy-start | bytes 98308
  67.9 2.9 %copy-start.1 = (f32[1,32]{1,0:T(1,128)S(1)}, f32[1,32]{1,0:T(1,128)}, u32[]{:S(2)}) copy-start(f32[1,32]{1,0:T(1,128)} %get-tuple-element.8) | copy-start | bytes 388
